TPU v7x, 32 devices: a whole 2x2x4 slice. The times are simulated.
32 devices in a mesh: dp: 8 (over y, x, core), mp: 4 (over z).
Axes of the slice: x: 2, y: 2, z: 4, core: 2. Of those that a mesh axis runs over, the one named last changes fastest.
Arguments:
- slab_values: bfloat16 [32, 32, 2048], P(('dp', 'mp')), may hold values from -6 to 6
- row_ids: int32 [32, 32, 32], P(('dp', 'mp')), may hold values from 0 to 4095, as said below
- peer_counts: int32 [32, 32], P(('dp', 'mp')), may hold values from 1 to 32, as said below
- lookup_slots: int32 [8192, 16], P(('dp', 'mp')), may hold values from 0 to 1023, as said below
- labels: int32 [8192], P('dp'), may hold values 0 or 1
- sample_weight: float32 [8192], P('dp'), may hold values from 0.3 to 9
- weight_in: bfloat16 [1024, 8192], P(None, 'mp'), may hold values from -0.1875 to 0.1875
- bias_in: float32 [8192], P('mp'), may hold values from -3 to 3
- weight_out: bfloat16 [8192], P('mp'), may hold values from -0.0625 to 0.0625
- dense_accum: float32 [1024, 8192], P('dp', 'mp'), may hold values from 1e-08 to 1e-06
- table_rows: float32 [131072, 64], P(('dp', 'mp')), may hold values from -0.12 to 0.12
- table_accum: float32 [131072], P(('dp', 'mp')), may hold values from 1e-12 to 1e-05
Outputs:
- weight_new: bfloat16 [1024, 8192], P(None, 'mp')
- accum_new: float32 [1024, 8192], P('dp', 'mp')
- table_new: float32 [131072, 64], P(('dp', 'mp'))
- table_accum_new: float32 [131072], P(('dp', 'mp'))
Inputs may be any that keep to these rules, and one draw needn't show every extreme that they name: `row_ids`: the first peer_counts entries of each device's list for an owner are distinct rows of that owner's shard. `peer_counts`: some owner has 32 touched rows on every device, and some device has 32 touched rows of every owner. `lookup_slots`: below the sum of that device's peer_counts; every device has a lookup of its last touched row.
All inputs are finite; a program needn't handle non-finite values. No bound on the sum of `labels` on one device may be relied on, other than what follows from the above.
Results may differ from a plain program's by a relative error of at most 0.0034.
Values may be sent and summed in bfloat16 or wider, within the bound.
A program may use at most 128 MiB of HBM per device.

v0:
```python
import jax
import jax.numpy as jnp
from jax import lax
from jax.sharding import PartitionSpec as P

clip_norm = 1.0
dense_rate = 0.02
table_rate = 0.5
adagrad_eps = 1e-10


def slot_index(compact, counts, capacity):
    slot_ends = jnp.cumsum(counts)
    owner_index = jnp.sum((compact[..., None] >= slot_ends).astype(jnp.int32), axis=-1)
    slot_starts = slot_ends - counts
    owner_match = owner_index[..., None] == jnp.arange(counts.shape[0], dtype=jnp.int32)
    owner_begin = jnp.sum(jnp.where(owner_match, slot_starts, 0), axis=-1)
    return owner_index * capacity + compact - owner_begin


def body(
    slab_values,
    row_ids,
    peer_counts,
    lookup_slots,
    labels,
    sample_weight,
    weight_in,
    bias_in,
    weight_out,
    dense_accum,
    table_rows,
    table_accum,
):
    peers = peer_counts.shape[1]
    capacity = row_ids.shape[2]
    emb_width = slab_values.shape[2] // capacity
    batch = lookup_slots.shape[0]
    features = lookup_slots.shape[1]
    index = slot_index(lookup_slots, peer_counts[0], capacity)
    slab_view = slab_values[0].reshape(peers * capacity, emb_width)
    pooled = slab_view[index].reshape(batch, features * emb_width)
    group = lax.all_gather(pooled, "mp", axis=0, tiled=True)
    act = jnp.dot(group, weight_in, preferred_element_type=jnp.float32) + bias_in
    hidden = jax.nn.silu(act).astype(jnp.bfloat16)
    logit = lax.psum(jnp.dot(hidden, weight_out, preferred_element_type=jnp.float32), "mp")
    dlogit = sample_weight * (jax.nn.sigmoid(logit) - labels.astype(jnp.float32))
    sigma = jax.nn.sigmoid(act)
    dact = (
        dlogit[:, None]
        * weight_out.astype(jnp.float32)[None, :]
        * sigma
        * (1.0 + act * (1.0 - sigma))
    ).astype(jnp.bfloat16)
    dpooled = lax.psum_scatter(
        lax.dot_general(
            dact, weight_in, (((1,), (1,)), ((), ())), preferred_element_type=jnp.float32
        ),
        "mp",
        scatter_dimension=0,
        tiled=True,
    )
    slot_grad = jax.ops.segment_sum(
        dpooled.reshape(batch * features, emb_width),
        index.reshape(-1),
        num_segments=peers * capacity,
    )
    grad_in = lax.dot_general(
        group, dact, (((0,), (0,)), ((), ())), preferred_element_type=jnp.float32
    )
    grad_bias = jnp.sum(dact.astype(jnp.float32), axis=0)
    grad_out = jnp.dot(dlogit, hidden.astype(jnp.float32), precision=lax.Precision.HIGHEST)
    first_group = (lax.axis_index("dp") == 0).astype(jnp.float32)
    own_rows = dense_accum.shape[0]
    row_start = lax.axis_index("dp") * own_rows
    grad_rows = lax.psum_scatter(grad_in, "dp", scatter_dimension=0, tiled=True)
    grad_bias, grad_out = lax.psum((grad_bias, grad_out), "dp")
    dense_square = jnp.sum(grad_rows * grad_rows)
    dense_square = dense_square + first_group * (
        jnp.sum(grad_bias * grad_bias) + jnp.sum(grad_out * grad_out)
    )
    total = lax.psum(dense_square + jnp.sum(slot_grad * slot_grad), ("dp", "mp"))
    scale = clip_norm / jnp.maximum(jnp.sqrt(total), clip_norm)
    clipped = scale * grad_rows
    accum_new = dense_accum + clipped * clipped
    weight_part = lax.dynamic_slice_in_dim(weight_in, row_start, own_rows, 0).astype(jnp.float32)
    updated = (weight_part - dense_rate * clipped / (jnp.sqrt(accum_new) + adagrad_eps)).astype(
        jnp.bfloat16
    )
    weight_new = lax.all_gather(updated, "dp", axis=0, tiled=True)
    row_values = row_ids[0].astype(jnp.float32)
    outgoing = (scale * slot_grad).reshape(peers, capacity * emb_width)
    arrived, arrived_rows = (
        lax.all_to_all(outgoing, ("dp", "mp"), split_axis=0, concat_axis=0, tiled=True),
        lax.all_to_all(row_values, ("dp", "mp"), split_axis=0, concat_axis=0, tiled=True),
    )
    received = jax.ops.segment_sum(
        arrived.reshape(-1, emb_width),
        arrived_rows.reshape(-1).astype(jnp.int32),
        num_segments=table_rows.shape[0],
    )
    table_accum_new = table_accum + jnp.mean(received * received, axis=1)
    table_new = table_rows - table_rate * received / (
        jnp.sqrt(table_accum_new)[:, None] + adagrad_eps
    )
    return (weight_new, accum_new, table_new, table_accum_new)


def solution(mesh):
    placed = (
        P(("dp", "mp"), None, None),
        P(("dp", "mp"), None, None),
        P(("dp", "mp"), None),
        P(("dp", "mp"), None),
        P("dp"),
        P("dp"),
        P(None, "mp"),
        P("mp"),
        P("mp"),
        P("dp", "mp"),
        P(("dp", "mp"), None),
        P(("dp", "mp")),
    )
    return jax.shard_map(
        body,
        mesh=mesh,
        in_specs=placed,
        out_specs=(P(None, "mp"), P("dp", "mp"), P(("dp", "mp"), None), P(("dp", "mp"))),
        check_vma=False,
    )
```

profile of v0, /device:TPU:0, one launch (start us, length us, event | category | flops | bytes accessed | tf_op | source)
XLA Modules:
  0.0 362.3 jit_solution(8915836303579359678)
XLA Ops:
  12.0 12.1 %gather_fusion = bf16[4096,64]{1,0:T(8,128)(2,1)S(1)} fusion(bf16[1024,64]{1,0:T(8,128)(2,1)S(1)} %reshape_squeeze.3, s32[4096]{0:T(1024)S(1)} %broadcast_clamp_fusion), kind=kCustom, calls=%fused_computation | custom fusion | bytes 1064960 | tf_op jit(solution)/shard_map/gather | solution.py:42
  25.7 48.5 %all-gather.3.cloned.1.call-done = bf16[1024,1024]{1,0:T(8,128)(2,1)} async-done(((bf16[256,1024]{1,0:T(8,128)(2,1)}), bf16[1024,1024]{1,0:T(8,128)(2,1)}) %all-gather.3.cloned.1.call-update) | async-done | bytes 2097168 | tf_op jit(solution)/shard_map/all_gather | solution.py:43
  74.2 11.2 %multiply_convert_fusion.1 = (bf16[1024,2048]{1,0:T(8,128)(2,1)S(1)}, f32[1024,2048]{1,0:T(8,128)}) fusion(f32[2048]{0:T(1024)S(1)} %copy-done.7, bf16[1024,1024]{1,0:T(8,128)(2,1)} %all-gather.3.cloned.1.call-done, bf16[1024,2048]{1,0:T(8,128)(2,1)} %param.18), kind=kOutput, calls=%fused_computation.5 | convolution fusion | flops 4307550208 | bytes 18882560 | tf_op jit(solution)/shard_map/dot_general | solution.py:44
  88.5 9.7 %psum.28 = f32[1024]{0:T(1024)S(1)} all-reduce(f32[1024]{0:T(1024)S(1)} %bitcast.19), channel_id=1, replica_groups=mesh['dp'=8,'mp'=4] {'mp'}, use_global_device_ids=true, to_apply=%region_3.4 | all-reduce | flops 1024 | bytes 8192 | tf_op jit(solution)/shard_map/psum | solution.py:46
  98.2 6.1 %convert_reduce_fusion = (f32[2048]{0:T(1024)S(1)}, bf16[1024,2048]{1,0:T(8,128)(2,1)S(1)}) fusion(f32[1024,2048]{1,0:T(8,128)} %get-tuple-element.27, f32[2048]{0:T(1024)S(1)} %copy-done.7, f32[2048]{0:T(1024)S(1)} %convert_element_type.56, f32[1024]{0:T(1024)S(1)} %subtract_multiply_fusion), kind=kLoop, calls=%fused_computation.3 | loop fusion | flops 27260928 | bytes 12611584 | tf_op jit(solution)/shard_map/reduce_sum | solution.py:71
  104.4 2.0 copy-done.1
  106.4 6.1 %fusion.7 = f32[1024,1024]{1,0:T(8,128)} fusion(bf16[1024,2048]{1,0:T(8,128)(2,1)S(1)} %get-tuple-element.23, bf16[1024,2048]{1,0:T(8,128)(2,1)S(1)} %copy-done.3), kind=kOutput, calls=%fused_computation.34 | convolution fusion | flops 4294967296 | bytes 12582912 | tf_op jit(solution)/shard_map/dot_general | solution.py:56
  114.1 9.0 %fusion.5 = f32[1024,2048]{1,0:T(8,128)} fusion(bf16[1024,1024]{1,0:T(8,128)(2,1)S(1)} %copy-done.10, bf16[1024,2048]{1,0:T(8,128)(2,1)} %copy-done.1), kind=kOutput, calls=%fused_computation.32 | convolution fusion | flops 4294967296 | bytes 14680064 | tf_op jit(solution)/shard_map/dot_general | solution.py:68
  123.3 3.9 %fusion.6 = f32[1,2048]{1,0:T(1,128)S(1)} fusion(f32[1024,1]{0,1:T(1,128)S(1)} %bitcast.17, bf16[1024,2048]{1,0:T(8,128)(2,1)} %copy-done), kind=kOutput, calls=%fused_computation.33 | convolution fusion | flops 25165824 | bytes 4206592 | tf_op jit(solution)/shard_map/dot_general | solution.py:72
  127.2 22.8 %all-reduce = (f32[2048]{0:T(1024)S(1)}, f32[2048]{0:T(1024)S(1)}) all-reduce(f32[2048]{0:T(1024)S(1)} %get-tuple-element.22, f32[2048]{0:T(1024)S(1)} %bitcast.18), channel_id=1, replica_groups=mesh['dp'=8,'mp'=4] {'dp'}, use_global_device_ids=true, to_apply=%region_7.8 | all-reduce | flops 4096 | bytes 32768 | tf_op jit(solution)/shard_map/psum | solution.py:77
  151.9 35.8 %reduce-scatter.5.cloned.1.call-done = f32[256,1024]{1,0:T(8,128)} async-done(((f32[1024,1024]{1,0:T(8,128)}), f32[256,1024]{1,0:T(8,128)}) %reduce-scatter.5.cloned.1.call-update) | async-done | bytes 1048592 | tf_op jit(solution)/shard_map/reduce_scatter | solution.py:55
  189.4 22.5 %scatter_custom_fusion = f32[1024,64]{1,0:T(8,128)S(1)} fusion(s32[4096]{0:T(1024)S(1)} %reshape.94, f32[4096,64]{1,0:T(8,128)S(1)} %reshape.96, f32[]{:T(128)} %constant.19.clone.1), kind=kCustom, calls=%fused_computation.19 | custom fusion | flops 262144 | bytes 262148 | tf_op jit(solution)/shard_map/scatter-add | solution.py:63
  212.6 50.6 %reduce-scatter.3.cloned.1.call-done = f32[128,2048]{1,0:T(8,128)} async-done(((f32[1024,2048]{1,0:T(8,128)}), f32[128,2048]{1,0:T(8,128)}) %reduce-scatter.3.cloned.1.call-update) | async-done | bytes 1048592 | tf_op jit(solution)/shard_map/reduce_scatter | solution.py:76
  263.2 2.1 multiply_reduce_fusion.1
  266.6 39.3 %psum.31 = f32[]{:T(128)} all-reduce(f32[]{:T(128)S(6)} %add.86), channel_id=1, replica_groups=mesh['dp'=8,'mp'=4] {'dp','mp'}, use_global_device_ids=true, to_apply=%region_14.15 | all-reduce | flops 1 | bytes 8 | tf_op jit(solution)/shard_map/psum | solution.py:82
  306.6 3.4 subtract_convert_fusion
  310.7 5.6 %all-to-all-start = ((f32[32,1,32]{2,1,0:T(1,128)}), f32[32,1,32]{2,1,0:T(1,128)S(1)}, u32[]{:S(2)}, u32[]{:S(2)}) async-start(f32[32,1,32]{2,1,0:T(1,128)} %bitcast.5), calls=%async_computation.2 | async-start | bytes 32768 | tf_op jit(solution)/shard_map/all_to_all | solution.py:95
  317.3 6.1 %all-to-all-done = f32[32,1,32]{2,1,0:T(1,128)S(1)} async-done(((f32[32,1,32]{2,1,0:T(1,128)}), f32[32,1,32]{2,1,0:T(1,128)S(1)}, u32[]{:S(2)}, u32[]{:S(2)}) %all-to-all-start) | async-done | bytes 4128 | tf_op jit(solution)/shard_map/all_to_all | solution.py:95
  323.4 2.8 all-to-all-start.1
  328.3 8.0 %all-to-all-done.1 = f32[32,1,2048]{2,1,0:T(1,128)S(1)} async-done(((f32[32,1,2048]{2,1,0:T(1,128)}), f32[32,1,2048]{2,1,0:T(1,128)S(1)}, u32[]{:S(2)}, u32[]{:S(2)}) %all-to-all-start.1) | async-done | bytes 262176 | tf_op jit(solution)/shard_map/all_to_all | solution.py:94
  337.1 6.5 %scatter_custom_fusion.1 = f32[4096,64]{1,0:T(8,128)S(1)} fusion(s32[1024]{0:T(1024)S(1)} %reshape.102, f32[1024,64]{1,0:T(8,128)S(1)} %reshape.104, f32[]{:T(128)} %constant.19.clone.1), kind=kCustom, calls=%fused_computation.9 | custom fusion | flops 65536 | bytes 1048580 | tf_op jit(solution)/shard_map/scatter-add | solution.py:97
  344.9 2.9 divide_subtract_fusion
  347.8 3.1 copy.39
  350.9 4.8 %copy.41 = bf16[1024,2048]{1,0:T(8,128)(2,1)} copy(bf16[1024,2048]{1,0:T(8,128)(2,1)} %all-gather.5.cloned.1.call-done) | data formatting | bytes 8388608
  (61 shorter events, 20.2 us)
Async XLA Ops:
  7.2 67.0 %all-gather.3.cloned.1.call-start = ((), (), s32[]{:S(2)}) async-start(), calls=%async_computation.4 | async-start | bytes 2621440 | tf_op jit(solution)/shard_map/all_gather | solution.py:43
  11.9 13.8 %copy-start.4 = (bf16[2048]{0:T(1024)(128)(2,1)S(1)}, bf16[2048]{0:T(1024)(128)(2,1)}, u32[]{:S(2)}) copy-start(bf16[2048]{0:T(1024)(128)(2,1)} %param.20) | copy-start | bytes 12292
  12.0 62.2 %copy-start.7 = (f32[2048]{0:T(1024)S(1)}, f32[2048]{0:T(1024)}, u32[]{:S(2)}) copy-start(f32[2048]{0:T(1024)} %param.19) | copy-start | bytes 24580
  25.6 162.0 %reduce-scatter.5.cloned.1.call-start = ((), (), s32[]{:S(2)}) async-start(), calls=%async_computation.6 | async-start | bytes 5242880 | tf_op jit(solution)/shard_map/reduce_scatter | solution.py:55
  85.3 2.0 copy-start
  85.3 12.9 %copy-start.8 = (f32[1024]{0:T(1024)S(1)}, f32[1024]{0:T(1024)}, u32[]{:S(2)}) copy-start(f32[1024]{0:T(1024)} %param.17) | copy-start | bytes 12292
  85.3 12.9 %copy-start.9 = (s32[1024]{0:T(1024)S(1)}, s32[1024]{0:T(1024)}, u32[]{:S(2)}) copy-start(s32[1024]{0:T(1024)} %param.16) | copy-start | bytes 12292
  98.2 8.1 %copy-start.3 = (bf16[1024,2048]{1,0:T(8,128)(2,1)S(1)}, bf16[1024,2048]{1,0:T(8,128)(2,1)}, u32[]{:S(2)}) copy-start(bf16[1024,2048]{1,0:T(8,128)(2,1)} %param.18) | copy-start | bytes 12582916
  104.4 2.0 copy-start.1
  112.5 1.6 copy-start.10
  112.5 150.7 %reduce-scatter.3.cloned.1.call-start = ((), (), s32[]{:S(2)}) async-start(), calls=%async_computation.5 | async-start | bytes 9437184 | tf_op jit(solution)/shard_map/reduce_scatter | solution.py:76
  123.0 227.9 %all-gather.5.cloned.1.call-start = ((), (), s32[]{:S(2)}) async-start(), calls=%async_computation.7 | async-start | bytes 4718592 | tf_op jit(solution)/shard_map/all_gather | solution.py:90
  189.4 120.7 %copy-start.5 = (s32[1,32,32]{2,1,0:T(8,128)S(1)}, s32[1,32,32]{2,1,0:T(8,128)}, u32[]{:S(2)}) copy-start(s32[1,32,32]{2,1,0:T(8,128)} %param.13) | copy-start | bytes 12292
  212.6 113.6 %copy-start.2 = (f32[4096,64]{0,1:T(8,128)S(1)}, f32[4096,64]{0,1:T(8,128)}, u32[]{:S(2)}) copy-start(f32[4096,64]{0,1:T(8,128)} %param.22) | copy-start | bytes 3145732
  310.7 12.7 %all-to-all-start = ((f32[32,1,32]{2,1,0:T(1,128)}), f32[32,1,32]{2,1,0:T(1,128)S(1)}, u32[]{:S(2)}, u32[]{:S(2)}) async-start(f32[32,1,32]{2,1,0:T(1,128)} %bitcast.5), calls=%async_computation.2 | async-start | bytes 32768 | tf_op jit(solution)/shard_map/all_to_all | solution.py:95
  323.4 12.9 %all-to-all-start.1 = ((f32[32,1,2048]{2,1,0:T(1,128)}), f32[32,1,2048]{2,1,0:T(1,128)S(1)}, u32[]{:S(2)}, u32[]{:S(2)}) async-start(f32[32,1,2048]{2,1,0:T(1,128)} %all_to_all.13), calls=%async_computation.3 | async-start | bytes 524288 | tf_op jit(solution)/shard_map/all_to_all | solution.py:94
  326.2 18.1 %copy-start.6 = (f32[4096]{0:T(1024)S(1)}, f32[4096]{0:T(1024)}, u32[]{:S(2)}) copy-start(f32[4096]{0:T(1024)} %param.23) | copy-start | bytes 49156
Sparse Core Ops, SparseCore 0:
  25.8 48.3 all-gather.2
  112.6 74.9 reduce-scatter.4
  191.1 72.0 reduce-scatter.2
  310.2 37.9 all-gather.4
where the time goes:
time: 363 us; the launch traced here: 362 us
  waiting for transfers between devices  149 us (41%)
  blocking collectives  71.8 us (20%)
  other arithmetic  50 us (14%)
  local copies, waits for them, and re-layouts  34.2 us (9%)
  matrix products  31.3 us (9%)
  between operations  17.4 us (5%)
  starting transfers between devices  8.71 us (2%)
    reduce_scatter x1, waiting for transfers between devices, body(): grad_rows = lax.psum_scatter(grad_in, 'dp', scatter_dimension=0, tiled=True)  50.6 us
    all_gather x1, waiting for transfers between devices, body(): group = lax.all_gather(pooled, 'mp', axis=0, tiled=True)  48.5 us
    psum x1, blocking collectives, body(): lax.psum(dense_square + jnp.sum(slot_grad * slot_grad), ('dp', 'mp'))  39.3 us
    reduce_scatter x1, waiting for transfers between devices, body(): lax.psum_scatter(lax.dot_general(dact, weight_in, (((1,), (1,)), ((), ())...  35.8 us
    psum x1, blocking collectives, body(): grad_bias, grad_out = lax.psum((grad_bias, grad_out), 'dp')  22.8 us
    scatter-add x1, other arithmetic, body(): jax.ops.segment_sum(dpooled.reshape(batch * features, emb_width), index.r...  22.5 us
    unnamed x26, local copies, waits for them, and re-layouts  15.2 us
    gather x1, local copies, waits for them, and re-layouts, body(): pooled = slab_view[index].reshape(batch, features * emb_width)  12.1 us
  transfers between devices with their start and end apart: 6, of which 5 were waited for; matrix products, arithmetic and copies ran while one was open for 15% of the time, Pallas kernels for 0%

commit v1 on v0

--- a/solution.py
+++ b/solution.py
@@ -79,7 +79,9 @@
     dense_square = dense_square + first_group * (
         jnp.sum(grad_bias * grad_bias) + jnp.sum(grad_out * grad_out)
     )
-    total = lax.psum(dense_square + jnp.sum(slot_grad * slot_grad), ("dp", "mp"))
+    x = dense_square + jnp.sum(slot_grad * slot_grad)
+    parts = lax.all_gather(x, ("dp", "mp"), axis=0, tiled=False)
+    total = parts.sum(axis=0)
     scale = clip_norm / jnp.maximum(jnp.sqrt(total), clip_norm)
     clipped = scale * grad_rows
     accum_new = dense_accum + clipped * clipped

time: 363 us -> 364 us (level)
    psum x1 -> x0, blocking collectives: 39.3 us -> none  [body(): lax.psum(dense_square + jnp.sum(slot_grad * slot_grad), ('dp', 'mp'))]
    unnamed x0 -> x1, blocking collectives: none -> 39.2 us
    unnamed x26 -> x28, local copies, waits for them, and re-layouts: 15.2 us -> 15.3 us
where the time goes in v1:
time: 364 us; the launch traced here: 363 us
  waiting for transfers between devices  149 us (41%)
  blocking collectives  71.7 us (20%)
  other arithmetic  50.6 us (14%)
  local copies, waits for them, and re-layouts  34.3 us (9%)
  matrix products  31.3 us (9%)
  between operations  17.4 us (5%)
  starting transfers between devices  8.52 us (2%)
    reduce_scatter x1, waiting for transfers between devices, body(): grad_rows = lax.psum_scatter(grad_in, 'dp', scatter_dimension=0, tiled=True)  50.6 us
    all_gather x1, waiting for transfers between devices, body(): group = lax.all_gather(pooled, 'mp', axis=0, tiled=True)  48.5 us
    unnamed x1, blocking collectives  39.2 us
    reduce_scatter x1, waiting for transfers between devices, body(): lax.psum_scatter(lax.dot_general(dact, weight_in, (((1,), (1,)), ((), ())...  35.8 us
    psum x1, blocking collectives, body(): grad_bias, grad_out = lax.psum((grad_bias, grad_out), 'dp')  22.8 us
    scatter-add x1, other arithmetic, body(): jax.ops.segment_sum(dpooled.reshape(batch * features, emb_width), index.r...  22.5 us
    unnamed x28, local copies, waits for them, and re-layouts  15.3 us
    gather x1, local copies, waits for them, and re-layouts, body(): pooled = slab_view[index].reshape(batch, features * emb_width)  12.1 us
  transfers between devices with their start and end apart: 6, of which 5 were waited for; matrix products, arithmetic and copies ran while one was open for 15% of the time, Pallas kernels for 0%

profile of v1, /device:TPU:0, one launch (start us, length us, event | category | flops | bytes accessed | tf_op | source)
XLA Modules:
  0.0 362.8 jit_solution(1748825777367017277)
XLA Ops:
  12.0 12.1 %gather_fusion = bf16[4096,64]{1,0:T(8,128)(2,1)S(1)} fusion(bf16[1024,64]{1,0:T(8,128)(2,1)S(1)} %reshape_squeeze.3, s32[4096]{0:T(1024)S(1)} %broadcast_clamp_fusion), kind=kCustom, calls=%fused_computation | custom fusion | bytes 1064960 | tf_op jit(solution)/shard_map/gather | solution.py:42
  25.7 48.5 %all-gather.3.cloned.1.call-done = bf16[1024,1024]{1,0:T(8,128)(2,1)} async-done(((bf16[256,1024]{1,0:T(8,128)(2,1)}), bf16[1024,1024]{1,0:T(8,128)(2,1)}) %all-gather.3.cloned.1.call-update) | async-done | bytes 2097168 | tf_op jit(solution)/shard_map/all_gather | solution.py:43
  74.2 11.2 %multiply_convert_fusion.1 = (bf16[1024,2048]{1,0:T(8,128)(2,1)S(1)}, f32[1024,2048]{1,0:T(8,128)}) fusion(f32[2048]{0:T(1024)S(1)} %copy-done.7, bf16[1024,1024]{1,0:T(8,128)(2,1)} %all-gather.3.cloned.1.call-done, bf16[1024,2048]{1,0:T(8,128)(2,1)} %param.18), kind=kOutput, calls=%fused_computation.5 | convolution fusion | flops 4307550208 | bytes 18882560 | tf_op jit(solution)/shard_map/dot_general | solution.py:44
  88.5 9.7 %psum.21 = f32[1024]{0:T(1024)S(1)} all-reduce(f32[1024]{0:T(1024)S(1)} %bitcast.20), channel_id=1, replica_groups=mesh['dp'=8,'mp'=4] {'mp'}, use_global_device_ids=true, to_apply=%region_3.4 | all-reduce | flops 1024 | bytes 8192 | tf_op jit(solution)/shard_map/psum | solution.py:46
  98.2 6.1 %convert_reduce_fusion = (f32[2048]{0:T(1024)S(1)}, bf16[1024,2048]{1,0:T(8,128)(2,1)S(1)}) fusion(f32[1024,2048]{1,0:T(8,128)} %get-tuple-element.27, f32[2048]{0:T(1024)S(1)} %copy-done.7, f32[2048]{0:T(1024)S(1)} %convert_element_type.56, f32[1024]{0:T(1024)S(1)} %subtract_multiply_fusion), kind=kLoop, calls=%fused_computation.3 | loop fusion | flops 27260928 | bytes 12611584 | tf_op jit(solution)/shard_map/reduce_sum | solution.py:71
  104.4 2.0 copy-done.1
  106.4 6.1 %fusion.7 = f32[1024,1024]{1,0:T(8,128)} fusion(bf16[1024,2048]{1,0:T(8,128)(2,1)S(1)} %get-tuple-element.23, bf16[1024,2048]{1,0:T(8,128)(2,1)S(1)} %copy-done.3), kind=kOutput, calls=%fused_computation.34 | convolution fusion | flops 4294967296 | bytes 12582912 | tf_op jit(solution)/shard_map/dot_general | solution.py:56
  114.1 9.0 %fusion.5 = f32[1024,2048]{1,0:T(8,128)} fusion(bf16[1024,1024]{1,0:T(8,128)(2,1)S(1)} %copy-done.10, bf16[1024,2048]{1,0:T(8,128)(2,1)} %copy-done.1), kind=kOutput, calls=%fused_computation.32 | convolution fusion | flops 4294967296 | bytes 14680064 | tf_op jit(solution)/shard_map/dot_general | solution.py:68
  123.3 3.9 %fusion.6 = f32[1,2048]{1,0:T(1,128)S(1)} fusion(f32[1024,1]{0,1:T(1,128)S(1)} %bitcast.18, bf16[1024,2048]{1,0:T(8,128)(2,1)} %copy-done), kind=kOutput, calls=%fused_computation.33 | convolution fusion | flops 25165824 | bytes 4206592 | tf_op jit(solution)/shard_map/dot_general | solution.py:72
  127.2 22.8 %all-reduce.1 = (f32[2048]{0:T(1024)S(1)}, f32[2048]{0:T(1024)S(1)}) all-reduce(f32[2048]{0:T(1024)S(1)} %get-tuple-element.22, f32[2048]{0:T(1024)S(1)} %bitcast.19), channel_id=1, replica_groups=mesh['dp'=8,'mp'=4] {'dp'}, use_global_device_ids=true, to_apply=%region_7.8 | all-reduce | flops 4096 | bytes 32768 | tf_op jit(solution)/shard_map/psum | solution.py:77
  151.9 35.8 %reduce-scatter.5.cloned.1.call-done = f32[256,1024]{1,0:T(8,128)} async-done(((f32[1024,1024]{1,0:T(8,128)}), f32[256,1024]{1,0:T(8,128)}) %reduce-scatter.5.cloned.1.call-update) | async-done | bytes 1048592 | tf_op jit(solution)/shard_map/reduce_scatter | solution.py:55
  189.4 22.5 %scatter_custom_fusion = f32[1024,64]{1,0:T(8,128)S(1)} fusion(s32[4096]{0:T(1024)S(1)} %reshape.94, f32[4096,64]{1,0:T(8,128)S(1)} %reshape.96, f32[]{:T(128)} %constant.19.clone.1), kind=kCustom, calls=%fused_computation.19 | custom fusion | flops 262144 | bytes 262148 | tf_op jit(solution)/shard_map/scatter-add | solution.py:63
  212.6 50.6 %reduce-scatter.3.cloned.1.call-done = f32[128,2048]{1,0:T(8,128)} async-done(((f32[1024,2048]{1,0:T(8,128)}), f32[128,2048]{1,0:T(8,128)}) %reduce-scatter.3.cloned.1.call-update) | async-done | bytes 1048592 | tf_op jit(solution)/shard_map/reduce_scatter | solution.py:76
  263.2 2.1 multiply_reduce_fusion.1
  266.7 39.2 %all-reduce = f32[32]{0:T(128)S(1)} all-reduce(f32[32]{0:T(128)S(1)} %dynamic-update-slice), channel_id=1, replica_groups=mesh['dp'=8,'mp'=4] {'dp','mp'}, use_global_device_ids=true, to_apply=%add | all-reduce | flops 32 | bytes 256
  307.3 3.4 subtract_convert_fusion
  311.3 5.4 %all-to-all-start = ((f32[32,1,32]{2,1,0:T(1,128)}), f32[32,1,32]{2,1,0:T(1,128)S(1)}, u32[]{:S(2)}, u32[]{:S(2)}) async-start(f32[32,1,32]{2,1,0:T(1,128)} %bitcast.6), calls=%async_computation.2 | async-start | bytes 32768 | tf_op jit(solution)/shard_map/all_to_all | solution.py:97
  317.8 6.1 %all-to-all-done = f32[32,1,32]{2,1,0:T(1,128)S(1)} async-done(((f32[32,1,32]{2,1,0:T(1,128)}), f32[32,1,32]{2,1,0:T(1,128)S(1)}, u32[]{:S(2)}, u32[]{:S(2)}) %all-to-all-start) | async-done | bytes 4128 | tf_op jit(solution)/shard_map/all_to_all | solution.py:97
  323.8 2.8 all-to-all-start.1
  328.7 8.0 %all-to-all-done.1 = f32[32,1,2048]{2,1,0:T(1,128)S(1)} async-done(((f32[32,1,2048]{2,1,0:T(1,128)}), f32[32,1,2048]{2,1,0:T(1,128)S(1)}, u32[]{:S(2)}, u32[]{:S(2)}) %all-to-all-start.1) | async-done | bytes 262176 | tf_op jit(solution)/shard_map/all_to_all | solution.py:96
  337.6 6.5 %scatter_custom_fusion.1 = f32[4096,64]{1,0:T(8,128)S(1)} fusion(s32[1024]{0:T(1024)S(1)} %reshape.102, f32[1024,64]{1,0:T(8,128)S(1)} %reshape.104, f32[]{:T(128)} %constant.19.clone.1), kind=kCustom, calls=%fused_computation.9 | custom fusion | flops 65536 | bytes 1048580 | tf_op jit(solution)/shard_map/scatter-add | solution.py:99
  345.4 2.9 divide_subtract_fusion
  348.3 3.1 copy.39
  351.4 4.8 %copy.42 = bf16[1024,2048]{1,0:T(8,128)(2,1)} copy(bf16[1024,2048]{1,0:T(8,128)(2,1)} %all-gather.5.cloned.1.call-done) | data formatting | bytes 8388608
  (64 shorter events, 20.9 us)
Async XLA Ops:
  7.2 67.0 %all-gather.3.cloned.1.call-start = ((), (), s32[]{:S(2)}) async-start(), calls=%async_computation.4 | async-start | bytes 2621440 | tf_op jit(solution)/shard_map/all_gather | solution.py:43
  11.9 13.8 %copy-start.4 = (bf16[2048]{0:T(1024)(128)(2,1)S(1)}, bf16[2048]{0:T(1024)(128)(2,1)}, u32[]{:S(2)}) copy-start(bf16[2048]{0:T(1024)(128)(2,1)} %param.20) | copy-start | bytes 12292
  12.0 62.2 %copy-start.7 = (f32[2048]{0:T(1024)S(1)}, f32[2048]{0:T(1024)}, u32[]{:S(2)}) copy-start(f32[2048]{0:T(1024)} %param.19) | copy-start | bytes 24580
  25.6 162.0 %reduce-scatter.5.cloned.1.call-start = ((), (), s32[]{:S(2)}) async-start(), calls=%async_computation.6 | async-start | bytes 5242880 | tf_op jit(solution)/shard_map/reduce_scatter | solution.py:55
  85.3 2.0 copy-start
  85.3 12.9 %copy-start.8 = (f32[1024]{0:T(1024)S(1)}, f32[1024]{0:T(1024)}, u32[]{:S(2)}) copy-start(f32[1024]{0:T(1024)} %param.17) | copy-start | bytes 12292
  85.3 12.9 %copy-start.9 = (s32[1024]{0:T(1024)S(1)}, s32[1024]{0:T(1024)}, u32[]{:S(2)}) copy-start(s32[1024]{0:T(1024)} %param.16) | copy-start | bytes 12292
  98.2 8.1 %copy-start.3 = (bf16[1024,2048]{1,0:T(8,128)(2,1)S(1)}, bf16[1024,2048]{1,0:T(8,128)(2,1)}, u32[]{:S(2)}) copy-start(bf16[1024,2048]{1,0:T(8,128)(2,1)} %param.18) | copy-start | bytes 12582916
  104.4 2.0 copy-start.1
  112.5 1.6 copy-start.10
  112.5 150.7 %reduce-scatter.3.cloned.1.call-start = ((), (), s32[]{:S(2)}) async-start(), calls=%async_computation.5 | async-start | bytes 9437184 | tf_op jit(solution)/shard_map/reduce_scatter | solution.py:76
  123.0 228.4 %all-gather.5.cloned.1.call-start = ((), (), s32[]{:S(2)}) async-start(), calls=%async_computation.7 | async-start | bytes 4718592 | tf_op jit(solution)/shard_map/all_gather | solution.py:92
  189.4 121.4 %copy-start.5 = (s32[1,32,32]{2,1,0:T(8,128)S(1)}, s32[1,32,32]{2,1,0:T(8,128)}, u32[]{:S(2)}) copy-start(s32[1,32,32]{2,1,0:T(8,128)} %param.13) | copy-start | bytes 12292
  212.6 114.1 %copy-start.2 = (f32[4096,64]{0,1:T(8,128)S(1)}, f32[4096,64]{0,1:T(8,128)}, u32[]{:S(2)}) copy-start(f32[4096,64]{0,1:T(8,128)} %param.22) | copy-start | bytes 3145732
  311.3 12.5 %all-to-all-start = ((f32[32,1,32]{2,1,0:T(1,128)}), f32[32,1,32]{2,1,0:T(1,128)S(1)}, u32[]{:S(2)}, u32[]{:S(2)}) async-start(f32[32,1,32]{2,1,0:T(1,128)} %bitcast.6), calls=%async_computation.2 | async-start | bytes 32768 | tf_op jit(solution)/shard_map/all_to_all | solution.py:97
  323.8 12.9 %all-to-all-start.1 = ((f32[32,1,2048]{2,1,0:T(1,128)}), f32[32,1,2048]{2,1,0:T(1,128)S(1)}, u32[]{:S(2)}, u32[]{:S(2)}) async-start(f32[32,1,2048]{2,1,0:T(1,128)} %all_to_all.13), calls=%async_computation.3 | async-start | bytes 524288 | tf_op jit(solution)/shard_map/all_to_all | solution.py:96
  326.7 18.1 %copy-start.6 = (f32[4096]{0:T(1024)S(1)}, f32[4096]{0:T(1024)}, u32[]{:S(2)}) copy-start(f32[4096]{0:T(1024)} %param.23) | copy-start | bytes 49156
Sparse Core Ops, SparseCore 0:
  25.8 48.3 all-gather.2
  112.6 74.9 reduce-scatter.4
  191.1 72.0 reduce-scatter.2
  310.8 37.7 all-gather.4
